TPU v7x, 32 devices: a whole 2x2x4 slice. The times are simulated.
32 devices in a mesh: gx: 2 (over x), gy: 4 (over y, core), ha: 4 (over z).
Axes of the slice: x: 2, y: 2, z: 4, core: 2. Of those that a mesh axis runs over, the one named last changes fastest.
Arguments:
- global_state: float32 [8, 60, 16, 16], P(None, 'ha', 'gx', 'gy'), may hold values from -6 to 6
- crm_state: float32 [8, 60, 16, 1024], P(None, 'ha', 'gx', 'gy'), may hold values from -6 to 6
- mixing: float32 [8, 8], replicated, may hold values from -2 to 2
- substeps: int32 [16, 16], P('gx', 'gy'), may hold values from 1 to 8
- assignment: int32 [16, 16], P('gx', 'gy'), may hold values from 0 to 31, as said below
Outputs:
- new_global: float32 [8, 60, 16, 16], P(None, 'ha', 'gx', 'gy')
- new_crm: float32 [8, 60, 16384], P(None, None, ('gx', 'gy', 'ha'))
Inputs may be any that keep to these rules, and one draw needn't show every extreme that they name: `assignment`: within each tile of 8 x 4 columns every value 0 .. 31 appears once; value // 8 is the helper index, value % 8 the slot on that helper.
All inputs are finite; a program needn't handle non-finite values.
Results may differ from a plain program's by a relative error of at most 0.0003.
Values sent between devices are 32-bit elements; how exact they have to be, the bound alone decides.
A program may use at most 64 MiB of HBM per device.

v0:
```python
import jax
import jax.numpy as jnp
from jax import lax
from jax.sharding import PartitionSpec as P

MAXSUB = 8
GSUB = 4
HIGH = lax.Precision.HIGHEST


def extended(cells, sides, width):
    for axis, dim in sides:
        count = lax.axis_size(axis)
        head = lax.slice_in_dim(cells, 0, width, axis=dim)
        tail = lax.slice_in_dim(cells, cells.shape[dim] - width, cells.shape[dim], axis=dim)
        cells = jnp.concatenate(
            [
                lax.ppermute(tail, axis, [(i, (i + 1) % count) for i in range(count)]),
                cells,
                lax.ppermute(head, axis, [((i + 1) % count, i) for i in range(count)]),
            ],
            axis=dim,
        )
    return cells


def global_operator(padded):
    center = padded[:, :, 1:-1, 1:-1]
    east = padded[:, :, 2:, 1:-1]
    west = padded[:, :, :-2, 1:-1]
    north = padded[:, :, 1:-1, 2:]
    south = padded[:, :, 1:-1, :-2]
    return (
        0.2 * (east + west + north + south - 4.0 * center)
        - 0.15 * (east - west)
        - 0.15 * (north - south)
    )


def crm_update(state, pushed, mixing):
    lateral = jnp.roll(state, 1, axis=3) + jnp.roll(state, -1, axis=3) - 2.0 * state
    upper = jnp.concatenate([state[:, :1], state[:, :-1]], axis=1)
    lower = jnp.concatenate([state[:, 1:], state[:, -1:]], axis=1)
    coupling = jnp.einsum("gf,flsc->glsc", mixing, jnp.tanh(state), precision=HIGH)
    return state + 0.1 * (1.0 * lateral + 0.5 * (upper + lower - 2.0 * state) + pushed + coupling)


def advance(states, pushed, slot_counts, mixing):

    def one_step(index, state):
        updated = crm_update(state, pushed, mixing)
        return jnp.where((index < slot_counts)[:, None], updated, state)

    return lax.fori_loop(0, MAXSUB, one_step, states)


def on_device(global_state, crm_state, mixing, substeps, assignment):
    current = global_state
    for substep in range(GSUB // 2):
        padded = extended(current, (("gx", 2), ("gy", 3)), 2)
        middle = padded[:, :, 1:-1, 1:-1] + 0.5 * global_operator(padded)
        current = middle[:, :, 1:-1, 1:-1] + 0.5 * global_operator(middle)
    forcing = (current - global_state) / (0.5 * GSUB)
    tile_x, tile_y = assignment.shape
    columns = tile_x * tile_y
    helpers = lax.axis_size("ha")
    per_helper = columns // helpers
    fields, level_part = (crm_state.shape[0], crm_state.shape[1])
    width = crm_state.shape[3] // tile_y
    global_fields = forcing.shape[0]
    onehot = (
        assignment.reshape(columns)[:, None] == jnp.arange(columns, dtype=jnp.int32)[None, :]
    ).astype(jnp.float32)
    helper = lax.axis_index("ha")
    own_slots = lax.dynamic_slice_in_dim(onehot, helper * per_helper, per_helper, 1)
    local_states = crm_state.reshape(fields, level_part, columns, width)
    slotted = jnp.einsum("flxc,xj->fljc", local_states, onehot, precision=HIGH)
    pushes = jnp.einsum(
        "glx,xj->glj", forcing.reshape(global_fields, level_part, columns), onehot, precision=HIGH
    )
    pushes = pushes.reshape(global_fields, level_part, columns, 1)
    states, pushed = (
        lax.all_to_all(slotted, "ha", split_axis=2, concat_axis=1, tiled=True),
        lax.all_to_all(pushes, "ha", split_axis=2, concat_axis=1, tiled=True),
    )
    slot_counts = jnp.dot(
        substeps.reshape(1, columns).astype(jnp.float32), own_slots, precision=HIGH
    )
    slot_counts = slot_counts.reshape(per_helper).astype(jnp.int32)
    advanced = advance(states, pushed, slot_counts, mixing)
    tendency = jnp.mean(advanced - states, axis=3)
    returned = lax.all_to_all(tendency, "ha", split_axis=1, concat_axis=2, tiled=True)
    placed = jnp.dot(returned.reshape(fields * level_part, columns), onehot.T, precision=HIGH)
    new_global = current + placed.reshape(fields, level_part, tile_x, tile_y)
    levels_all = advanced.shape[1]
    return (new_global, advanced.reshape(fields, levels_all, per_helper * width))


def solution(mesh):
    in_specs = (
        P(None, "ha", "gx", "gy"),
        P(None, "ha", "gx", "gy"),
        P(),
        P("gx", "gy"),
        P("gx", "gy"),
    )
    out_specs = (P(None, "ha", "gx", "gy"), P(None, None, ("gx", "gy", "ha")))
    return jax.shard_map(
        on_device, mesh=mesh, in_specs=in_specs, out_specs=out_specs, check_vma=False
    )
```

profile of v0, /device:TPU:0, one launch (start us, length us, event | category | flops | bytes accessed | tf_op | source)
XLA Modules:
  0.0 139.4 jit_solution(3381811293322487794)
XLA Ops:
  0.6 0.9 copy.92
  1.6 3.0 %collective-permute-start = (f32[8,15,2,4]{1,2,3,0:T(2,128)S(1)}, f32[8,15,2,4]{1,2,3,0:T(2,128)S(1)}, u32[]{:S(2)}, u32[]{:S(2)}) collective-permute-start(f32[8,15,2,4]{1,2,3,0:T(2,128)S(1)} %get-tuple-element.155), channel_id=1, source_target_pairs={{0,16},{16,0},{1,17},{17,1},{2,18},{18,2},{3,19},{19,3},{4,20},{20... | collective-permute-start | bytes 11528 | tf_op jit(solution)/shard_map/ppermute | solution.py:18
  4.7 1.8 %collective-permute-done = f32[8,15,2,4]{1,2,3,0:T(2,128)S(1)} collective-permute-done((f32[8,15,2,4]{1,2,3,0:T(2,128)S(1)}, f32[8,15,2,4]{1,2,3,0:T(2,128)S(1)}, u32[]{:S(2)}, u32[]{:S(2)}) %collective-permute-start) | collective-permute-done | bytes 3872 | tf_op jit(solution)/shard_map/ppermute | solution.py:18
  6.5 2.0 %collective-permute-done.1 = f32[8,15,2,4]{1,2,3,0:T(2,128)S(1)} collective-permute-done((f32[8,15,2,4]{1,2,3,0:T(2,128)S(1)}, f32[8,15,2,4]{1,2,3,0:T(2,128)S(1)}, u32[]{:S(2)}, u32[]{:S(2)}) %collective-permute-start.1) | collective-permute-done | bytes 3872 | tf_op jit(solution)/shard_map/ppermute | solution.py:20
  8.7 1.7 %collective-permute-start.3 = (f32[8,15,12,2]{1,2,3,0:T(8,128)S(1)}, f32[8,15,12,2]{1,2,3,0:T(8,128)S(1)}, u32[]{:S(2)}, u32[]{:S(2)}) collective-permute-start(f32[8,15,12,2]{1,2,3,0:T(8,128)S(1)} %get-tuple-element.152), channel_id=1, source_target_pairs={{4,0},{8,4},{12,8},{0,12},{5,1},{9,5},{13,9},{1,13},{6,2},{10,6},{... | collective-permute-start | bytes 34568 | tf_op jit(solution)/shard_map/ppermute | solution.py:20
  10.4 2.6 %collective-permute-done.2 = f32[8,15,12,2]{1,2,3,0:T(8,128)S(1)} collective-permute-done((f32[8,15,12,2]{1,2,3,0:T(8,128)S(1)}, f32[8,15,12,2]{1,2,3,0:T(8,128)S(1)}, u32[]{:S(2)}, u32[]{:S(2)}) %collective-permute-start.2) | collective-permute-done | bytes 11552 | tf_op jit(solution)/shard_map/ppermute | solution.py:18
  14.7 1.5 %collective-permute-start.5 = (f32[8,15,2,4]{1,2,3,0:T(2,128)S(1)}, f32[8,15,2,4]{1,2,3,0:T(2,128)S(1)}, u32[]{:S(2)}, u32[]{:S(2)}) collective-permute-start(f32[8,15,2,4]{1,2,3,0:T(2,128)S(1)} %get-tuple-element.154), channel_id=1, source_target_pairs={{16,0},{0,16},{17,1},{1,17},{18,2},{2,18},{19,3},{3,19},{20,4},{4,... | collective-permute-start | bytes 11528 | tf_op jit(solution)/shard_map/ppermute | solution.py:20
  16.2 2.0 %collective-permute-done.4 = f32[8,15,2,4]{1,2,3,0:T(2,128)S(1)} collective-permute-done((f32[8,15,2,4]{1,2,3,0:T(2,128)S(1)}, f32[8,15,2,4]{1,2,3,0:T(2,128)S(1)}, u32[]{:S(2)}, u32[]{:S(2)}) %collective-permute-start.4) | collective-permute-done | bytes 3872 | tf_op jit(solution)/shard_map/ppermute | solution.py:18
  19.9 1.6 %collective-permute-start.7 = (f32[8,15,12,2]{1,2,3,0:T(8,128)S(1)}, f32[8,15,12,2]{1,2,3,0:T(8,128)S(1)}, u32[]{:S(2)}, u32[]{:S(2)}) collective-permute-start(f32[8,15,12,2]{1,2,3,0:T(8,128)S(1)} %get-tuple-element.150), channel_id=1, source_target_pairs={{4,0},{8,4},{12,8},{0,12},{5,1},{9,5},{13,9},{1,13},{6,2},{10,6},{... | collective-permute-start | bytes 34568 | tf_op jit(solution)/shard_map/ppermute | solution.py:20
  22.0 2.4 %collective-permute-done.6 = f32[8,15,12,2]{1,2,3,0:T(8,128)S(1)} collective-permute-done((f32[8,15,12,2]{1,2,3,0:T(8,128)}, f32[8,15,12,2]{1,2,3,0:T(8,128)S(1)}, u32[]{:S(2)}, u32[]{:S(2)}) %collective-permute-start.6) | collective-permute-done | bytes 11552 | tf_op jit(solution)/shard_map/ppermute | solution.py:18
  25.9 0.8 reshape.67
  26.7 4.9 %all-to-all-start.1 = ((f32[4,1,960]{2,1,0:T(1,128)}), f32[4,1,960]{2,1,0:T(1,128)S(1)}, u32[]{:S(2)}, u32[]{:S(2)}) async-start(f32[4,1,960]{2,1,0:T(1,128)} %reshape.67), calls=%async_computation.1 | async-start | bytes 32768 | tf_op jit(solution)/shard_map/all_to_all | solution.py:84
  31.5 1.1 convolution_bitcast_fusion
  32.7 1.1 copy.133
  33.9 2.3 %reshape.65 = f32[4,1,61440]{2,1,0:T(1,128)} reshape(f32[32,15,8,64]{3,2,1,0:T(8,128)S(1)} %bitcast.68) | data formatting | bytes 1966080
  36.2 1.0 all-to-all-done.1
  37.2 4.1 %all-to-all-start = ((f32[4,1,61440]{2,1,0:T(1,128)}), f32[4,1,61440]{2,1,0:T(1,128)S(1)}, u32[]{:S(2)}, u32[]{:S(2)}) async-start(f32[4,1,61440]{2,1,0:T(1,128)} %reshape.65), calls=%async_computation | async-start | bytes 1966080 | tf_op jit(solution)/shard_map/all_to_all | solution.py:83
  43.5 22.7 %all-to-all-done = f32[4,1,61440]{2,1,0:T(1,128)S(1)} async-done(((f32[4,1,61440]{2,1,0:T(1,128)}), f32[4,1,61440]{2,1,0:T(1,128)S(1)}, u32[]{:S(2)}, u32[]{:S(2)}) %all-to-all-start) | async-done | bytes 983072 | tf_op jit(solution)/shard_map/all_to_all | solution.py:83
  66.2 3.5 %reduce = f32[4,61440]{1,0:T(4,128)S(1)} reduce(f32[4,1,61440]{2,1,0:T(1,128)S(1)} %all-to-all-done, f32[]{:T(128)} %broadcast.101), dimensions={1}, to_apply=%all_to_all.37.reduce_sub_computation | reduce | bytes 1966084 | tf_op jit(solution)/shard_map/all_to_all | solution.py:83
  69.7 1.0 reshape.66
  71.1 1.1 copy-done
  72.2 53.0 %while.13 = (s32[]{:T(128)}, f32[8,60,8,64]{3,0,2,1:T(8,128)S(1)}, s32[8]{0:T(128)S(1)}, f32[8,60,8,1]{0,2,1,3:T(8,128)S(1)}, f32[8,8]{1,0:T(8,128)S(1)}, /*index=5*/s32[]{:T(128)}) while((s32[]{:T(128)}, f32[8,60,8,64]{3,0,2,1:T(8,128)S(1)}, s32[8]{0:T(128)S(1)}, f32[8,60,8,1]{0,2,1,3:T(8,128)S(1)}, f32[8,8]{1,0:T(8,128)S(1)}, ...), condition=%wide.region_1.2_spmd, body=%wide.region_0.1_spmd.sunk | while | flops 27525128 | bytes 15744385 | solution.py:54
  72.9 0.8 fusion.44
  73.7 0.8 fusion.43
  74.4 4.4 %add_select_fusion.2 = f32[8,60,8,64]{3,0,2,1:T(8,128)S(1)} fusion(f32[8,60,8,64]{3,0,2,1:T(8,128)S(1)} %copy.145, f32[8,60,8,63]{3,0,2,1:T(8,128)S(1)} %get-tuple-element.196, f32[8,60,8,1]{3,0,2,1:T(8,128)S(1)} %get-tuple-element.197, f32[8,60,8,1]{3,0,2,1:T(8,128)S(1)} %get-tuple-element.198, f32[8,60,8,63]{3,0,2,1:T(8,128)S(1)} %get-tuple-element.199, ...), kind=kOutput, calls=%fused_computation.clone.1 | convolution fusion | flops 27525120 | bytes 5913864 | tf_op jit(solution)/shard_map/while/body/eval_jaxpr/gf,flsc->glsc/dot_general | solution.py:44
  79.5 0.8 fusion.44
  80.3 0.8 fusion.43
  81.1 4.4 %add_select_fusion.2 = f32[8,60,8,64]{3,0,2,1:T(8,128)S(1)} fusion(f32[8,60,8,64]{3,0,2,1:T(8,128)S(1)} %copy.145, f32[8,60,8,63]{3,0,2,1:T(8,128)S(1)} %get-tuple-element.196, f32[8,60,8,1]{3,0,2,1:T(8,128)S(1)} %get-tuple-element.197, f32[8,60,8,1]{3,0,2,1:T(8,128)S(1)} %get-tuple-element.198, f32[8,60,8,63]{3,0,2,1:T(8,128)S(1)} %get-tuple-element.199, ...), kind=kOutput, calls=%fused_computation.clone.1 | convolution fusion | flops 27525120 | bytes 5913864 | tf_op jit(solution)/shard_map/while/body/eval_jaxpr/gf,flsc->glsc/dot_general | solution.py:44
  86.9 0.8 fusion.43
  87.7 4.4 %add_select_fusion.2 = f32[8,60,8,64]{3,0,2,1:T(8,128)S(1)} fusion(f32[8,60,8,64]{3,0,2,1:T(8,128)S(1)} %copy.145, f32[8,60,8,63]{3,0,2,1:T(8,128)S(1)} %get-tuple-element.196, f32[8,60,8,1]{3,0,2,1:T(8,128)S(1)} %get-tuple-element.197, f32[8,60,8,1]{3,0,2,1:T(8,128)S(1)} %get-tuple-element.198, f32[8,60,8,63]{3,0,2,1:T(8,128)S(1)} %get-tuple-element.199, ...), kind=kOutput, calls=%fused_computation.clone.1 | convolution fusion | flops 27525120 | bytes 5913864 | tf_op jit(solution)/shard_map/while/body/eval_jaxpr/gf,flsc->glsc/dot_general | solution.py:44
  92.8 0.8 fusion.44
  93.5 0.8 fusion.43
  94.3 4.4 %add_select_fusion.2 = f32[8,60,8,64]{3,0,2,1:T(8,128)S(1)} fusion(f32[8,60,8,64]{3,0,2,1:T(8,128)S(1)} %copy.145, f32[8,60,8,63]{3,0,2,1:T(8,128)S(1)} %get-tuple-element.196, f32[8,60,8,1]{3,0,2,1:T(8,128)S(1)} %get-tuple-element.197, f32[8,60,8,1]{3,0,2,1:T(8,128)S(1)} %get-tuple-element.198, f32[8,60,8,63]{3,0,2,1:T(8,128)S(1)} %get-tuple-element.199, ...), kind=kOutput, calls=%fused_computation.clone.1 | convolution fusion | flops 27525120 | bytes 5913864 | tf_op jit(solution)/shard_map/while/body/eval_jaxpr/gf,flsc->glsc/dot_general | solution.py:44
  99.4 0.8 fusion.44
  100.2 0.8 fusion.43
  101.0 4.4 %add_select_fusion.2 = f32[8,60,8,64]{3,0,2,1:T(8,128)S(1)} fusion(f32[8,60,8,64]{3,0,2,1:T(8,128)S(1)} %copy.145, f32[8,60,8,63]{3,0,2,1:T(8,128)S(1)} %get-tuple-element.196, f32[8,60,8,1]{3,0,2,1:T(8,128)S(1)} %get-tuple-element.197, f32[8,60,8,1]{3,0,2,1:T(8,128)S(1)} %get-tuple-element.198, f32[8,60,8,63]{3,0,2,1:T(8,128)S(1)} %get-tuple-element.199, ...), kind=kOutput, calls=%fused_computation.clone.1 | convolution fusion | flops 27525120 | bytes 5913864 | tf_op jit(solution)/shard_map/while/body/eval_jaxpr/gf,flsc->glsc/dot_general | solution.py:44
  106.8 0.8 fusion.43
  107.6 4.4 %add_select_fusion.2 = f32[8,60,8,64]{3,0,2,1:T(8,128)S(1)} fusion(f32[8,60,8,64]{3,0,2,1:T(8,128)S(1)} %copy.145, f32[8,60,8,63]{3,0,2,1:T(8,128)S(1)} %get-tuple-element.196, f32[8,60,8,1]{3,0,2,1:T(8,128)S(1)} %get-tuple-element.197, f32[8,60,8,1]{3,0,2,1:T(8,128)S(1)} %get-tuple-element.198, f32[8,60,8,63]{3,0,2,1:T(8,128)S(1)} %get-tuple-element.199, ...), kind=kOutput, calls=%fused_computation.clone.1 | convolution fusion | flops 27525120 | bytes 5913864 | tf_op jit(solution)/shard_map/while/body/eval_jaxpr/gf,flsc->glsc/dot_general | solution.py:44
  113.4 0.8 fusion.43
  114.2 4.4 %add_select_fusion.2 = f32[8,60,8,64]{3,0,2,1:T(8,128)S(1)} fusion(f32[8,60,8,64]{3,0,2,1:T(8,128)S(1)} %copy.145, f32[8,60,8,63]{3,0,2,1:T(8,128)S(1)} %get-tuple-element.196, f32[8,60,8,1]{3,0,2,1:T(8,128)S(1)} %get-tuple-element.197, f32[8,60,8,1]{3,0,2,1:T(8,128)S(1)} %get-tuple-element.198, f32[8,60,8,63]{3,0,2,1:T(8,128)S(1)} %get-tuple-element.199, ...), kind=kOutput, calls=%fused_computation.clone.1 | convolution fusion | flops 27525120 | bytes 5913864 | tf_op jit(solution)/shard_map/while/body/eval_jaxpr/gf,flsc->glsc/dot_general | solution.py:44
  120.1 0.8 fusion.43
  120.8 4.4 %add_select_fusion.2 = f32[8,60,8,64]{3,0,2,1:T(8,128)S(1)} fusion(f32[8,60,8,64]{3,0,2,1:T(8,128)S(1)} %copy.145, f32[8,60,8,63]{3,0,2,1:T(8,128)S(1)} %get-tuple-element.196, f32[8,60,8,1]{3,0,2,1:T(8,128)S(1)} %get-tuple-element.197, f32[8,60,8,1]{3,0,2,1:T(8,128)S(1)} %get-tuple-element.198, f32[8,60,8,63]{3,0,2,1:T(8,128)S(1)} %get-tuple-element.199, ...), kind=kOutput, calls=%fused_computation.clone.1 | convolution fusion | flops 27525120 | bytes 5913864 | tf_op jit(solution)/shard_map/while/body/eval_jaxpr/gf,flsc->glsc/dot_general | solution.py:44
  125.2 2.1 %subtract_reduce_fusion = f32[8,60,8]{0,2,1:T(8,128)S(1)} fusion(f32[8,60,8,64]{3,0,2,1:T(8,128)S(1)} %get-tuple-element.96, f32[8,60,8,64]{3,0,2,1:T(8,128)} %bitcast.65), kind=kLoop, calls=%fused_computation.14 | loop fusion | flops 487680 | bytes 1981440 | tf_op jit(solution)/shard_map/reduce_sum | solution.py:91
  127.7 0.8 reshape.69
  128.5 3.3 %all-to-all-start.2 = ((f32[4,1,960]{2,1,0:T(1,128)}), f32[4,1,960]{2,1,0:T(1,128)S(1)}, u32[]{:S(2)}, u32[]{:S(2)}) async-start(f32[4,1,960]{2,1,0:T(1,128)} %reshape.69), calls=%async_computation.2 | async-start | bytes 32768 | tf_op jit(solution)/shard_map/all_to_all | solution.py:92
  131.8 1.7 %copy.112 = f32[8,60,8,64]{3,2,0,1:T(8,128)} copy(f32[8,60,8,64]{3,0,2,1:T(8,128)S(1)} %get-tuple-element.96) | data formatting | bytes 1966080 | tf_op jit(solution)/shard_map/while | solution.py:54
  133.5 2.6 %reshape.56 = f32[8,60,512]{2,0,1:T(8,128)} reshape(f32[8,60,8,64]{3,2,0,1:T(8,128)} %copy.112) | data formatting | bytes 1966080 | tf_op jit(solution)/shard_map/reshape | solution.py:96
  136.1 1.2 all-to-all-done.2
  (92 shorter events, 18.7 us)
Async XLA Ops:
  1.6 4.9 %collective-permute-start = (f32[8,15,2,4]{1,2,3,0:T(2,128)S(1)}, f32[8,15,2,4]{1,2,3,0:T(2,128)S(1)}, u32[]{:S(2)}, u32[]{:S(2)}) collective-permute-start(f32[8,15,2,4]{1,2,3,0:T(2,128)S(1)} %get-tuple-element.155), channel_id=1, source_target_pairs={{0,16},{16,0},{1,17},{17,1},{2,18},{18,2},{3,19},{19,3},{4,20},{20... | collective-permute-start | bytes 11528 | tf_op jit(solution)/shard_map/ppermute | solution.py:18
  4.6 3.9 %collective-permute-start.1 = (f32[8,15,2,4]{1,2,3,0:T(2,128)S(1)}, f32[8,15,2,4]{1,2,3,0:T(2,128)S(1)}, u32[]{:S(2)}, u32[]{:S(2)}) collective-permute-start(f32[8,15,2,4]{1,2,3,0:T(2,128)S(1)} %get-tuple-element.156), channel_id=1, source_target_pairs={{16,0},{0,16},{17,1},{1,17},{18,2},{2,18},{19,3},{3,19},{20,4},{4,... | collective-permute-start | bytes 11528 | tf_op jit(solution)/shard_map/ppermute | solution.py:20
  8.6 4.4 %collective-permute-start.2 = (f32[8,15,12,2]{1,2,3,0:T(8,128)S(1)}, f32[8,15,12,2]{1,2,3,0:T(8,128)S(1)}, u32[]{:S(2)}, u32[]{:S(2)}) collective-permute-start(f32[8,15,12,2]{1,2,3,0:T(8,128)S(1)} %get-tuple-element.151), channel_id=1, source_target_pairs={{0,4},{4,8},{8,12},{12,0},{1,5},{5,9},{9,13},{13,1},{2,6},{6,10},{... | collective-permute-start | bytes 34568 | tf_op jit(solution)/shard_map/ppermute | solution.py:18
  8.7 4.8 %collective-permute-start.3 = (f32[8,15,12,2]{1,2,3,0:T(8,128)S(1)}, f32[8,15,12,2]{1,2,3,0:T(8,128)S(1)}, u32[]{:S(2)}, u32[]{:S(2)}) collective-permute-start(f32[8,15,12,2]{1,2,3,0:T(8,128)S(1)} %get-tuple-element.152), channel_id=1, source_target_pairs={{4,0},{8,4},{12,8},{0,12},{5,1},{9,5},{13,9},{1,13},{6,2},{10,6},{... | collective-permute-start | bytes 34568 | tf_op jit(solution)/shard_map/ppermute | solution.py:20
  13.6 7.9 %copy-start.4 = (s32[8,4]{0,1:T(4,128)S(1)}, s32[8,4]{0,1:T(4,128)}, u32[]{:S(2)}) copy-start(s32[8,4]{0,1:T(4,128)} %param.11) | copy-start | bytes 388
  13.6 8.1 %copy-start.1 = (f32[8,15,8,256]{3,2,1,0:T(8,128)S(1)}, f32[8,15,8,256]{3,2,1,0:T(8,128)}, u32[]{:S(2)}) copy-start(f32[8,15,8,256]{3,2,1,0:T(8,128)} %param.8) | copy-start | bytes 2949124
  14.1 4.1 %collective-permute-start.4 = (f32[8,15,2,4]{1,2,3,0:T(2,128)S(1)}, f32[8,15,2,4]{1,2,3,0:T(2,128)S(1)}, u32[]{:S(2)}, u32[]{:S(2)}) collective-permute-start(f32[8,15,2,4]{1,2,3,0:T(2,128)S(1)} %get-tuple-element.153), channel_id=1, source_target_pairs={{0,16},{16,0},{1,17},{17,1},{2,18},{18,2},{3,19},{19,3},{4,20},{20... | collective-permute-start | bytes 11528 | tf_op jit(solution)/shard_map/ppermute | solution.py:18
  14.7 4.3 %collective-permute-start.5 = (f32[8,15,2,4]{1,2,3,0:T(2,128)S(1)}, f32[8,15,2,4]{1,2,3,0:T(2,128)S(1)}, u32[]{:S(2)}, u32[]{:S(2)}) collective-permute-start(f32[8,15,2,4]{1,2,3,0:T(2,128)S(1)} %get-tuple-element.154), channel_id=1, source_target_pairs={{16,0},{0,16},{17,1},{1,17},{18,2},{2,18},{19,3},{3,19},{20,4},{4,... | collective-permute-start | bytes 11528 | tf_op jit(solution)/shard_map/ppermute | solution.py:20
  19.7 4.6 %collective-permute-start.6 = (f32[8,15,12,2]{1,2,3,0:T(8,128)}, f32[8,15,12,2]{1,2,3,0:T(8,128)S(1)}, u32[]{:S(2)}, u32[]{:S(2)}) collective-permute-start(f32[8,15,12,2]{1,2,3,0:T(8,128)} %get-tuple-element.149), channel_id=1, source_target_pairs={{0,4},{4,8},{8,12},{12,0},{1,5},{5,9},{9,13},{13,1},{2,6},{6,10},{... | collective-permute-start | bytes 34568 | tf_op jit(solution)/shard_map/ppermute | solution.py:18
  19.9 4.9 %collective-permute-start.7 = (f32[8,15,12,2]{1,2,3,0:T(8,128)S(1)}, f32[8,15,12,2]{1,2,3,0:T(8,128)S(1)}, u32[]{:S(2)}, u32[]{:S(2)}) collective-permute-start(f32[8,15,12,2]{1,2,3,0:T(8,128)S(1)} %get-tuple-element.150), channel_id=1, source_target_pairs={{4,0},{8,4},{12,8},{0,12},{5,1},{9,5},{13,9},{1,13},{6,2},{10,6},{... | collective-permute-start | bytes 34568 | tf_op jit(solution)/shard_map/ppermute | solution.py:20
  22.0 3.3 %copy-start.2 = (f32[8,15,8,4]{1,3,2,0:T(4,128)S(1)}, f32[8,15,8,4]{1,3,2,0:T(4,128)}, u32[]{:S(2)}) copy-start(f32[8,15,8,4]{1,3,2,0:T(4,128)} %param.7) | copy-start | bytes 46084
  26.7 10.5 %all-to-all-start.1 = ((f32[4,1,960]{2,1,0:T(1,128)}), f32[4,1,960]{2,1,0:T(1,128)S(1)}, u32[]{:S(2)}, u32[]{:S(2)}) async-start(f32[4,1,960]{2,1,0:T(1,128)} %reshape.67), calls=%async_computation.1 | async-start | bytes 32768 | tf_op jit(solution)/shard_map/all_to_all | solution.py:84
  33.9 7.4 %copy-start.5 = (s32[8,4]{0,1:T(4,128)S(1)}, s32[8,4]{0,1:T(4,128)}, u32[]{:S(2)}) copy-start(s32[8,4]{0,1:T(4,128)} %param.10) | copy-start | bytes 388
  37.2 29.0 %all-to-all-start = ((f32[4,1,61440]{2,1,0:T(1,128)}), f32[4,1,61440]{2,1,0:T(1,128)S(1)}, u32[]{:S(2)}, u32[]{:S(2)}) async-start(f32[4,1,61440]{2,1,0:T(1,128)} %reshape.65), calls=%async_computation | async-start | bytes 1966080 | tf_op jit(solution)/shard_map/all_to_all | solution.py:83
  70.9 1.3 copy-start
  70.9 1.3 copy-start.3
  128.5 8.8 %all-to-all-start.2 = ((f32[4,1,960]{2,1,0:T(1,128)}), f32[4,1,960]{2,1,0:T(1,128)S(1)}, u32[]{:S(2)}, u32[]{:S(2)}) async-start(f32[4,1,960]{2,1,0:T(1,128)} %reshape.69), calls=%async_computation.2 | async-start | bytes 32768 | tf_op jit(solution)/shard_map/all_to_all | solution.py:92
where the time goes:
time: 140 us; the launch traced here: 139 us
  waiting for transfers between devices  37.3 us (27%)
  matrix products  37 us (26%)
  local copies, waits for them, and re-layouts  34.2 us (24%)
  starting transfers between devices  21 us (15%)
  other arithmetic  8.49 us (6%)
    dot_general x8, matrix products, crm_update(): jnp.einsum('gf,flsc->glsc', mixing, jnp.tanh(state), precision=HIGH)  35.1 us
    all_to_all x1, waiting for transfers between devices, on_device(): lax.all_to_all(slotted, 'ha', split_axis=2, concat_axis=1, tiled=True)  22.7 us
    slice x16, local copies, waits for them, and re-layouts, crm_update(): jnp.roll(state, -1, axis=3)  12.2 us
    ppermute x4, waiting for transfers between devices, extended(): lax.ppermute(tail, axis, [(i, (i + 1) % count) for i in range(count)])  8.83 us
    unnamed x22, local copies, waits for them, and re-layouts  8.09 us
    ppermute x4, starting transfers between devices, extended(): lax.ppermute(head, axis, [((i + 1) % count, i) for i in range(count)])  4.93 us
    all_to_all x1, starting transfers between devices, on_device(): lax.all_to_all(pushes, 'ha', split_axis=2, concat_axis=1, tiled=True)  4.86 us
    all_to_all x1, starting transfers between devices, on_device(): lax.all_to_all(slotted, 'ha', split_axis=2, concat_axis=1, tiled=True)  4.12 us
  transfers between devices with their start and end apart: 11, of which 11 were waited for; matrix products, arithmetic and copies ran while one was open for 8% of the time, Pallas kernels for 0%

commit v1 on v0

--- a/solution.py
+++ b/solution.py
@@ -80,7 +80,10 @@
     )
     pushes = pushes.reshape(global_fields, level_part, columns, 1)
     states, pushed = (
-        lax.all_to_all(slotted, "ha", split_axis=2, concat_axis=1, tiled=True),
+        jnp.concatenate(
+            lax.all_to_all(jnp.stack(jnp.split(slotted, lax.axis_size("ha"), axis=2)), "ha", 0, 0),
+            axis=1,
+        ),
         lax.all_to_all(pushes, "ha", split_axis=2, concat_axis=1, tiled=True),
     )
     slot_counts = jnp.dot(

time: 140 us -> 140 us (level)
  waiting for transfers between devices: 37.3 us -> 35.5 us
  other arithmetic: 8.49 us -> 10.2 us
    ppermute x4, waiting for transfers between devices: 8.83 us -> 6.3 us  [extended(): lax.ppermute(tail, axis, [(i, (i + 1) % count) for i in range(count)])]
    while x2 -> x3, local copies, waits for them, and re-layouts: 2.02 us -> 3.16 us  [advance(): return lax.fori_loop(0, MAXSUB, one_step, states)]
    unnamed x22 -> x23, local copies, waits for them, and re-layouts: 8.09 us -> 7.67 us
  transfers between devices with their start and end apart: 11 -> 11, of which waited for: 11 -> 11; matrix products, arithmetic and copies ran while one was open for 8% -> 10% of each run, Pallas kernels for 0% -> 0%
where the time goes in v1:
time: 140 us; the launch traced here: 139 us
  matrix products  37.1 us (26%)
  waiting for transfers between devices  35.5 us (25%)
  local copies, waits for them, and re-layouts  34.5 us (25%)
  starting transfers between devices  20.4 us (15%)
  other arithmetic  10.2 us (7%)
    dot_general x8, matrix products, crm_update(): jnp.einsum('gf,flsc->glsc', mixing, jnp.tanh(state), precision=HIGH)  35.2 us
    all_to_all x1, waiting for transfers between devices, on_device(): lax.all_to_all(jnp.stack(jnp.split(slotted, lax.axis_size('ha'), axis=2))...  22.2 us
    slice x16, local copies, waits for them, and re-layouts, crm_update(): jnp.roll(state, -1, axis=3)  12.2 us
    unnamed x23, local copies, waits for them, and re-layouts  7.67 us
    ppermute x4, waiting for transfers between devices, extended(): lax.ppermute(tail, axis, [(i, (i + 1) % count) for i in range(count)])  6.3 us
    ppermute x4, starting transfers between devices, extended(): lax.ppermute(head, axis, [((i + 1) % count, i) for i in range(count)])  4.94 us
    all_to_all x1, starting transfers between devices, on_device(): lax.all_to_all(pushes, 'ha', split_axis=2, concat_axis=1, tiled=True)  4.69 us
    slice x16, local copies, waits for them, and re-layouts, crm_update(): lower = jnp.concatenate([state[:, 1:], state[:, -1:]], axis=1)  4.03 us
  transfers between devices with their start and end apart: 11, of which 11 were waited for; matrix products, arithmetic and copies ran while one was open for 10% of the time, Pallas kernels for 0%

profile of v1, /device:TPU:0, one launch (start us, length us, event | category | flops | bytes accessed | tf_op | source)
XLA Modules:
  0.0 139.1 jit_solution(1636751220639650904)
XLA Ops:
  0.6 1.0 copy.75
  1.7 3.0 %collective-permute-start = (f32[8,15,2,4]{1,2,3,0:T(2,128)S(1)}, f32[8,15,2,4]{1,2,3,0:T(2,128)S(1)}, u32[]{:S(2)}, u32[]{:S(2)}) collective-permute-start(f32[8,15,2,4]{1,2,3,0:T(2,128)S(1)} %get-tuple-element.157), channel_id=1, source_target_pairs={{0,16},{16,0},{1,17},{17,1},{2,18},{18,2},{3,19},{19,3},{4,20},{20... | collective-permute-start | bytes 11528 | tf_op jit(solution)/shard_map/ppermute | solution.py:18
  4.8 1.8 %collective-permute-done = f32[8,15,2,4]{1,2,3,0:T(2,128)S(1)} collective-permute-done((f32[8,15,2,4]{1,2,3,0:T(2,128)S(1)}, f32[8,15,2,4]{1,2,3,0:T(2,128)S(1)}, u32[]{:S(2)}, u32[]{:S(2)}) %collective-permute-start) | collective-permute-done | bytes 3872 | tf_op jit(solution)/shard_map/ppermute | solution.py:18
  6.6 2.0 %collective-permute-done.1 = f32[8,15,2,4]{1,2,3,0:T(2,128)S(1)} collective-permute-done((f32[8,15,2,4]{1,2,3,0:T(2,128)S(1)}, f32[8,15,2,4]{1,2,3,0:T(2,128)S(1)}, u32[]{:S(2)}, u32[]{:S(2)}) %collective-permute-start.1) | collective-permute-done | bytes 3872 | tf_op jit(solution)/shard_map/ppermute | solution.py:20
  9.4 1.7 %collective-permute-start.3 = (f32[8,15,12,2]{1,2,3,0:T(8,128)S(1)}, f32[8,15,12,2]{1,2,3,0:T(8,128)S(1)}, u32[]{:S(2)}, u32[]{:S(2)}) collective-permute-start(f32[8,15,12,2]{1,2,3,0:T(8,128)S(1)} %get-tuple-element.154), channel_id=1, source_target_pairs={{4,0},{8,4},{12,8},{0,12},{5,1},{9,5},{13,9},{1,13},{6,2},{10,6},{... | collective-permute-start | bytes 34568 | tf_op jit(solution)/shard_map/ppermute | solution.py:20
  12.3 1.7 %collective-permute-done.2 = f32[8,15,12,2]{1,2,3,0:T(8,128)S(1)} collective-permute-done((f32[8,15,12,2]{1,2,3,0:T(8,128)}, f32[8,15,12,2]{1,2,3,0:T(8,128)S(1)}, u32[]{:S(2)}, u32[]{:S(2)}) %collective-permute-start.2) | collective-permute-done | bytes 11552 | tf_op jit(solution)/shard_map/ppermute | solution.py:18
  15.6 1.5 %collective-permute-start.5 = (f32[8,15,2,4]{1,2,3,0:T(2,128)S(1)}, f32[8,15,2,4]{1,2,3,0:T(2,128)S(1)}, u32[]{:S(2)}, u32[]{:S(2)}) collective-permute-start(f32[8,15,2,4]{1,2,3,0:T(2,128)S(1)} %get-tuple-element.156), channel_id=1, source_target_pairs={{16,0},{0,16},{17,1},{1,17},{18,2},{2,18},{19,3},{3,19},{20,4},{4,... | collective-permute-start | bytes 11528 | tf_op jit(solution)/shard_map/ppermute | solution.py:20
  17.1 1.1 convolution_bitcast_fusion
  18.3 1.1 collective-permute-done.4
  20.3 1.6 %collective-permute-start.7 = (f32[8,15,12,2]{1,2,3,0:T(8,128)S(1)}, f32[8,15,12,2]{1,2,3,0:T(8,128)S(1)}, u32[]{:S(2)}, u32[]{:S(2)}) collective-permute-start(f32[8,15,12,2]{1,2,3,0:T(8,128)S(1)} %get-tuple-element.152), channel_id=1, source_target_pairs={{4,0},{8,4},{12,8},{0,12},{5,1},{9,5},{13,9},{1,13},{6,2},{10,6},{... | collective-permute-start | bytes 34568 | tf_op jit(solution)/shard_map/ppermute | solution.py:20
  21.9 0.9 slice_bitcast_fusion.3
  22.8 1.7 %collective-permute-done.6 = f32[8,15,12,2]{1,2,3,0:T(8,128)S(1)} collective-permute-done((f32[8,15,12,2]{1,2,3,0:T(8,128)S(1)}, f32[8,15,12,2]{1,2,3,0:T(8,128)S(1)}, u32[]{:S(2)}, u32[]{:S(2)}) %collective-permute-start.6) | collective-permute-done | bytes 11552 | tf_op jit(solution)/shard_map/ppermute | solution.py:18
  27.6 4.7 %all-to-all-start.1 = ((f32[4,1,960]{2,1,0:T(1,128)}), f32[4,1,960]{2,1,0:T(1,128)S(1)}, u32[]{:S(2)}, u32[]{:S(2)}) async-start(f32[4,1,960]{2,1,0:T(1,128)} %reshape.75), calls=%async_computation.1 | async-start | bytes 32768 | tf_op jit(solution)/shard_map/all_to_all | solution.py:87
  32.3 1.2 pad_maximum_fusion
  33.5 2.3 %reshape.73 = f32[4,1,61440]{2,1,0:T(1,128)} reshape(f32[4,8,15,8,64]{4,3,2,1,0:T(8,128)S(1)} %pad_maximum_fusion) | data formatting | bytes 1966080
  35.8 2.2 %all-to-all-done.1 = f32[4,1,960]{2,1,0:T(1,128)S(1)} async-done(((f32[4,1,960]{2,1,0:T(1,128)}), f32[4,1,960]{2,1,0:T(1,128)S(1)}, u32[]{:S(2)}, u32[]{:S(2)}) %all-to-all-start.1) | async-done | bytes 15392 | tf_op jit(solution)/shard_map/all_to_all | solution.py:87
  38.0 3.7 %all-to-all-start = ((f32[4,1,61440]{2,1,0:T(1,128)}), f32[4,1,61440]{2,1,0:T(1,128)S(1)}, u32[]{:S(2)}, u32[]{:S(2)}) async-start(f32[4,1,61440]{2,1,0:T(1,128)} %reshape.73), calls=%async_computation | async-start | bytes 1966080 | tf_op jit(solution)/shard_map/all_to_all | solution.py:84
  43.8 22.2 %all-to-all-done = f32[4,1,61440]{2,1,0:T(1,128)S(1)} async-done(((f32[4,1,61440]{2,1,0:T(1,128)}), f32[4,1,61440]{2,1,0:T(1,128)S(1)}, u32[]{:S(2)}, u32[]{:S(2)}) %all-to-all-start) | async-done | bytes 983072 | tf_op jit(solution)/shard_map/all_to_all | solution.py:84
  66.0 3.5 %reduce = f32[4,61440]{1,0:T(4,128)S(1)} reduce(f32[4,1,61440]{2,1,0:T(1,128)S(1)} %all-to-all-done, f32[]{:T(128)} %broadcast.101), dimensions={1}, to_apply=%all_to_all.27.reduce_sub_computation | reduce | bytes 1966084 | tf_op jit(solution)/shard_map/all_to_all | solution.py:84
  69.5 1.0 reshape.74
  70.6 1.1 copy.88
  71.9 53.0 %while.13 = (s32[]{:T(128)}, f32[8,60,8,64]{3,0,2,1:T(8,128)S(1)}, s32[8]{0:T(128)S(1)}, f32[8,60,8,1]{0,2,1,3:T(8,128)S(1)}, f32[8,8]{1,0:T(8,128)S(1)}, /*index=5*/s32[]{:T(128)}) while((s32[]{:T(128)}, f32[8,60,8,64]{3,0,2,1:T(8,128)S(1)}, s32[8]{0:T(128)S(1)}, f32[8,60,8,1]{0,2,1,3:T(8,128)S(1)}, f32[8,8]{1,0:T(8,128)S(1)}, ...), condition=%wide.region_1.2_spmd, body=%wide.region_0.1_spmd.sunk | while | flops 27525128 | bytes 15744385 | solution.py:54
  72.6 0.8 fusion.45
  73.3 0.8 fusion.44
  74.1 4.4 %add_select_fusion.2 = f32[8,60,8,64]{3,0,2,1:T(8,128)S(1)} fusion(f32[8,60,8,64]{3,0,2,1:T(8,128)S(1)} %copy.130, f32[8,60,8,63]{3,0,2,1:T(8,128)S(1)} %get-tuple-element.198, f32[8,60,8,1]{3,0,2,1:T(8,128)S(1)} %get-tuple-element.199, f32[8,60,8,1]{3,0,2,1:T(8,128)S(1)} %get-tuple-element.200, f32[8,60,8,63]{3,0,2,1:T(8,128)S(1)} %get-tuple-element.201, ...), kind=kOutput, calls=%fused_computation.clone.1 | convolution fusion | flops 27525120 | bytes 5913864 | tf_op jit(solution)/shard_map/while/body/eval_jaxpr/gf,flsc->glsc/dot_general | solution.py:44
  79.2 0.8 fusion.45
  80.0 0.8 fusion.44
  80.8 4.4 %add_select_fusion.2 = f32[8,60,8,64]{3,0,2,1:T(8,128)S(1)} fusion(f32[8,60,8,64]{3,0,2,1:T(8,128)S(1)} %copy.130, f32[8,60,8,63]{3,0,2,1:T(8,128)S(1)} %get-tuple-element.198, f32[8,60,8,1]{3,0,2,1:T(8,128)S(1)} %get-tuple-element.199, f32[8,60,8,1]{3,0,2,1:T(8,128)S(1)} %get-tuple-element.200, f32[8,60,8,63]{3,0,2,1:T(8,128)S(1)} %get-tuple-element.201, ...), kind=kOutput, calls=%fused_computation.clone.1 | convolution fusion | flops 27525120 | bytes 5913864 | tf_op jit(solution)/shard_map/while/body/eval_jaxpr/gf,flsc->glsc/dot_general | solution.py:44
  86.6 0.8 fusion.44
  87.4 4.4 %add_select_fusion.2 = f32[8,60,8,64]{3,0,2,1:T(8,128)S(1)} fusion(f32[8,60,8,64]{3,0,2,1:T(8,128)S(1)} %copy.130, f32[8,60,8,63]{3,0,2,1:T(8,128)S(1)} %get-tuple-element.198, f32[8,60,8,1]{3,0,2,1:T(8,128)S(1)} %get-tuple-element.199, f32[8,60,8,1]{3,0,2,1:T(8,128)S(1)} %get-tuple-element.200, f32[8,60,8,63]{3,0,2,1:T(8,128)S(1)} %get-tuple-element.201, ...), kind=kOutput, calls=%fused_computation.clone.1 | convolution fusion | flops 27525120 | bytes 5913864 | tf_op jit(solution)/shard_map/while/body/eval_jaxpr/gf,flsc->glsc/dot_general | solution.py:44
  92.5 0.8 fusion.45
  93.3 0.8 fusion.44
  94.0 4.4 %add_select_fusion.2 = f32[8,60,8,64]{3,0,2,1:T(8,128)S(1)} fusion(f32[8,60,8,64]{3,0,2,1:T(8,128)S(1)} %copy.130, f32[8,60,8,63]{3,0,2,1:T(8,128)S(1)} %get-tuple-element.198, f32[8,60,8,1]{3,0,2,1:T(8,128)S(1)} %get-tuple-element.199, f32[8,60,8,1]{3,0,2,1:T(8,128)S(1)} %get-tuple-element.200, f32[8,60,8,63]{3,0,2,1:T(8,128)S(1)} %get-tuple-element.201, ...), kind=kOutput, calls=%fused_computation.clone.1 | convolution fusion | flops 27525120 | bytes 5913864 | tf_op jit(solution)/shard_map/while/body/eval_jaxpr/gf,flsc->glsc/dot_general | solution.py:44
  99.9 0.8 fusion.44
  100.7 4.4 %add_select_fusion.2 = f32[8,60,8,64]{3,0,2,1:T(8,128)S(1)} fusion(f32[8,60,8,64]{3,0,2,1:T(8,128)S(1)} %copy.130, f32[8,60,8,63]{3,0,2,1:T(8,128)S(1)} %get-tuple-element.198, f32[8,60,8,1]{3,0,2,1:T(8,128)S(1)} %get-tuple-element.199, f32[8,60,8,1]{3,0,2,1:T(8,128)S(1)} %get-tuple-element.200, f32[8,60,8,63]{3,0,2,1:T(8,128)S(1)} %get-tuple-element.201, ...), kind=kOutput, calls=%fused_computation.clone.1 | convolution fusion | flops 27525120 | bytes 5913864 | tf_op jit(solution)/shard_map/while/body/eval_jaxpr/gf,flsc->glsc/dot_general | solution.py:44
  106.5 0.8 fusion.44
  107.3 4.4 %add_select_fusion.2 = f32[8,60,8,64]{3,0,2,1:T(8,128)S(1)} fusion(f32[8,60,8,64]{3,0,2,1:T(8,128)S(1)} %copy.130, f32[8,60,8,63]{3,0,2,1:T(8,128)S(1)} %get-tuple-element.198, f32[8,60,8,1]{3,0,2,1:T(8,128)S(1)} %get-tuple-element.199, f32[8,60,8,1]{3,0,2,1:T(8,128)S(1)} %get-tuple-element.200, f32[8,60,8,63]{3,0,2,1:T(8,128)S(1)} %get-tuple-element.201, ...), kind=kOutput, calls=%fused_computation.clone.1 | convolution fusion | flops 27525120 | bytes 5913864 | tf_op jit(solution)/shard_map/while/body/eval_jaxpr/gf,flsc->glsc/dot_general | solution.py:44
  112.4 0.8 fusion.45
  113.1 0.8 fusion.44
  113.9 4.4 %add_select_fusion.2 = f32[8,60,8,64]{3,0,2,1:T(8,128)S(1)} fusion(f32[8,60,8,64]{3,0,2,1:T(8,128)S(1)} %copy.130, f32[8,60,8,63]{3,0,2,1:T(8,128)S(1)} %get-tuple-element.198, f32[8,60,8,1]{3,0,2,1:T(8,128)S(1)} %get-tuple-element.199, f32[8,60,8,1]{3,0,2,1:T(8,128)S(1)} %get-tuple-element.200, f32[8,60,8,63]{3,0,2,1:T(8,128)S(1)} %get-tuple-element.201, ...), kind=kOutput, calls=%fused_computation.clone.1 | convolution fusion | flops 27525120 | bytes 5913864 | tf_op jit(solution)/shard_map/while/body/eval_jaxpr/gf,flsc->glsc/dot_general | solution.py:44
  119.8 0.8 fusion.44
  120.6 4.4 %add_select_fusion.2 = f32[8,60,8,64]{3,0,2,1:T(8,128)S(1)} fusion(f32[8,60,8,64]{3,0,2,1:T(8,128)S(1)} %copy.130, f32[8,60,8,63]{3,0,2,1:T(8,128)S(1)} %get-tuple-element.198, f32[8,60,8,1]{3,0,2,1:T(8,128)S(1)} %get-tuple-element.199, f32[8,60,8,1]{3,0,2,1:T(8,128)S(1)} %get-tuple-element.200, f32[8,60,8,63]{3,0,2,1:T(8,128)S(1)} %get-tuple-element.201, ...), kind=kOutput, calls=%fused_computation.clone.1 | convolution fusion | flops 27525120 | bytes 5913864 | tf_op jit(solution)/shard_map/while/body/eval_jaxpr/gf,flsc->glsc/dot_general | solution.py:44
  125.0 2.2 %fusion.12 = f32[8,60,8]{2,1,0:T(8,128)S(1)} fusion(f32[8,60,8,64]{3,2,1,0:T(8,128)} %bitcast.67, f32[8,60,8,64]{3,0,2,1:T(8,128)S(1)} %get-tuple-element.96), kind=kLoop, calls=%fused_computation.16 | loop fusion | flops 487680 | bytes 1981440 | tf_op jit(solution)/shard_map/reduce_sum | solution.py:94
  127.5 0.8 reshape.77
  128.2 3.2 %all-to-all-start.2 = ((f32[4,1,960]{2,1,0:T(1,128)}), f32[4,1,960]{2,1,0:T(1,128)S(1)}, u32[]{:S(2)}, u32[]{:S(2)}) async-start(f32[4,1,960]{2,1,0:T(1,128)} %reshape.77), calls=%async_computation.2 | async-start | bytes 32768 | tf_op jit(solution)/shard_map/all_to_all | solution.py:95
  131.5 1.7 %copy.96 = f32[8,60,8,64]{3,2,0,1:T(8,128)} copy(f32[8,60,8,64]{3,0,2,1:T(8,128)S(1)} %get-tuple-element.96) | data formatting | bytes 1966080 | tf_op jit(solution)/shard_map/while | solution.py:54
  133.2 2.7 %reshape.64 = f32[8,60,512]{2,0,1:T(8,128)} reshape(f32[8,60,8,64]{3,2,0,1:T(8,128)} %copy.96) | data formatting | bytes 1966080 | tf_op jit(solution)/shard_map/reshape | solution.py:99
  135.9 1.2 all-to-all-done.2
  (95 shorter events, 20.5 us)
Async XLA Ops:
  0.6 11.3 %copy-start.1 = (f32[8,15,8,256]{3,2,1,0:T(8,128)S(1)}, f32[8,15,8,256]{3,2,1,0:T(8,128)}, u32[]{:S(2)}) copy-start(f32[8,15,8,256]{3,2,1,0:T(8,128)} %param.8) | copy-start | bytes 2949124
  1.7 4.9 %collective-permute-start = (f32[8,15,2,4]{1,2,3,0:T(2,128)S(1)}, f32[8,15,2,4]{1,2,3,0:T(2,128)S(1)}, u32[]{:S(2)}, u32[]{:S(2)}) collective-permute-start(f32[8,15,2,4]{1,2,3,0:T(2,128)S(1)} %get-tuple-element.157), channel_id=1, source_target_pairs={{0,16},{16,0},{1,17},{17,1},{2,18},{18,2},{3,19},{19,3},{4,20},{20... | collective-permute-start | bytes 11528 | tf_op jit(solution)/shard_map/ppermute | solution.py:18
  4.7 3.9 %collective-permute-start.1 = (f32[8,15,2,4]{1,2,3,0:T(2,128)S(1)}, f32[8,15,2,4]{1,2,3,0:T(2,128)S(1)}, u32[]{:S(2)}, u32[]{:S(2)}) collective-permute-start(f32[8,15,2,4]{1,2,3,0:T(2,128)S(1)} %get-tuple-element.158), channel_id=1, source_target_pairs={{16,0},{0,16},{17,1},{1,17},{18,2},{2,18},{19,3},{3,19},{20,4},{4,... | collective-permute-start | bytes 11528 | tf_op jit(solution)/shard_map/ppermute | solution.py:20
  9.4 4.6 %collective-permute-start.2 = (f32[8,15,12,2]{1,2,3,0:T(8,128)}, f32[8,15,12,2]{1,2,3,0:T(8,128)S(1)}, u32[]{:S(2)}, u32[]{:S(2)}) collective-permute-start(f32[8,15,12,2]{1,2,3,0:T(8,128)} %get-tuple-element.153), channel_id=1, source_target_pairs={{0,4},{4,8},{8,12},{12,0},{1,5},{5,9},{9,13},{13,1},{2,6},{6,10},{... | collective-permute-start | bytes 34568 | tf_op jit(solution)/shard_map/ppermute | solution.py:18
  9.4 5.0 %collective-permute-start.3 = (f32[8,15,12,2]{1,2,3,0:T(8,128)S(1)}, f32[8,15,12,2]{1,2,3,0:T(8,128)S(1)}, u32[]{:S(2)}, u32[]{:S(2)}) collective-permute-start(f32[8,15,12,2]{1,2,3,0:T(8,128)S(1)} %get-tuple-element.154), channel_id=1, source_target_pairs={{4,0},{8,4},{12,8},{0,12},{5,1},{9,5},{13,9},{1,13},{6,2},{10,6},{... | collective-permute-start | bytes 34568 | tf_op jit(solution)/shard_map/ppermute | solution.py:20
  15.0 4.3 %collective-permute-start.4 = (f32[8,15,2,4]{1,2,3,0:T(2,128)S(1)}, f32[8,15,2,4]{1,2,3,0:T(2,128)S(1)}, u32[]{:S(2)}, u32[]{:S(2)}) collective-permute-start(f32[8,15,2,4]{1,2,3,0:T(2,128)S(1)} %get-tuple-element.155), channel_id=1, source_target_pairs={{0,16},{16,0},{1,17},{17,1},{2,18},{18,2},{3,19},{19,3},{4,20},{20... | collective-permute-start | bytes 11528 | tf_op jit(solution)/shard_map/ppermute | solution.py:18
  15.6 4.4 %collective-permute-start.5 = (f32[8,15,2,4]{1,2,3,0:T(2,128)S(1)}, f32[8,15,2,4]{1,2,3,0:T(2,128)S(1)}, u32[]{:S(2)}, u32[]{:S(2)}) collective-permute-start(f32[8,15,2,4]{1,2,3,0:T(2,128)S(1)} %get-tuple-element.156), channel_id=1, source_target_pairs={{16,0},{0,16},{17,1},{1,17},{18,2},{2,18},{19,3},{3,19},{20,4},{4,... | collective-permute-start | bytes 11528 | tf_op jit(solution)/shard_map/ppermute | solution.py:20
  20.1 4.4 %collective-permute-start.6 = (f32[8,15,12,2]{1,2,3,0:T(8,128)S(1)}, f32[8,15,12,2]{1,2,3,0:T(8,128)S(1)}, u32[]{:S(2)}, u32[]{:S(2)}) collective-permute-start(f32[8,15,12,2]{1,2,3,0:T(8,128)S(1)} %get-tuple-element.151), channel_id=1, source_target_pairs={{0,4},{4,8},{8,12},{12,0},{1,5},{5,9},{9,13},{13,1},{2,6},{6,10},{... | collective-permute-start | bytes 34568 | tf_op jit(solution)/shard_map/ppermute | solution.py:18
  20.3 4.8 %collective-permute-start.7 = (f32[8,15,12,2]{1,2,3,0:T(8,128)S(1)}, f32[8,15,12,2]{1,2,3,0:T(8,128)S(1)}, u32[]{:S(2)}, u32[]{:S(2)}) collective-permute-start(f32[8,15,12,2]{1,2,3,0:T(8,128)S(1)} %get-tuple-element.152), channel_id=1, source_target_pairs={{4,0},{8,4},{12,8},{0,12},{5,1},{9,5},{13,9},{1,13},{6,2},{10,6},{... | collective-permute-start | bytes 34568 | tf_op jit(solution)/shard_map/ppermute | solution.py:20
  22.8 2.7 %copy-start.3 = (f32[8,15,8,4]{1,3,2,0:T(4,128)S(1)}, f32[8,15,8,4]{1,3,2,0:T(4,128)}, u32[]{:S(2)}) copy-start(f32[8,15,8,4]{1,3,2,0:T(4,128)} %param.7) | copy-start | bytes 46084
  27.6 10.3 %all-to-all-start.1 = ((f32[4,1,960]{2,1,0:T(1,128)}), f32[4,1,960]{2,1,0:T(1,128)S(1)}, u32[]{:S(2)}, u32[]{:S(2)}) async-start(f32[4,1,960]{2,1,0:T(1,128)} %reshape.75), calls=%async_computation.1 | async-start | bytes 32768 | tf_op jit(solution)/shard_map/all_to_all | solution.py:87
  33.5 8.2 %copy-start.6 = (s32[8,4]{0,1:T(4,128)S(1)}, s32[8,4]{0,1:T(4,128)}, u32[]{:S(2)}) copy-start(s32[8,4]{0,1:T(4,128)} %param.10) | copy-start | bytes 388
  38.0 28.1 %all-to-all-start = ((f32[4,1,61440]{2,1,0:T(1,128)}), f32[4,1,61440]{2,1,0:T(1,128)S(1)}, u32[]{:S(2)}, u32[]{:S(2)}) async-start(f32[4,1,61440]{2,1,0:T(1,128)} %reshape.73), calls=%async_computation | async-start | bytes 1966080 | tf_op jit(solution)/shard_map/all_to_all | solution.py:84
  70.6 1.3 copy-start
  70.6 1.3 copy-start.4
  128.2 8.8 %all-to-all-start.2 = ((f32[4,1,960]{2,1,0:T(1,128)}), f32[4,1,960]{2,1,0:T(1,128)S(1)}, u32[]{:S(2)}, u32[]{:S(2)}) async-start(f32[4,1,960]{2,1,0:T(1,128)} %reshape.77), calls=%async_computation.2 | async-start | bytes 32768 | tf_op jit(solution)/shard_map/all_to_all | solution.py:95
  133.2 5.0 %copy-start.2 = (f32[8,15,8,4]{1,2,3,0:T(8,128)S(1)}, f32[8,15,8,4]{1,2,3,0:T(8,128)}, u32[]{:S(2)}) copy-start(f32[8,15,8,4]{1,2,3,0:T(8,128)} %get-tuple-element.138) | copy-start | bytes 46084
  133.2 5.0 %copy-start.5 = (s32[8,4]{0,1:T(4,128)S(1)}, s32[8,4]{0,1:T(4,128)}, u32[]{:S(2)}) copy-start(s32[8,4]{0,1:T(4,128)} %param.11) | copy-start | bytes 388
